TPU v7x, 32 devices: a whole 2x2x4 slice. The times are simulated.
32 devices in a mesh: grp: 2 (over y), seq: 4 (over z), head: 4 (over x, core).
Axes of the slice: x: 2, y: 2, z: 4, core: 2. Of those that a mesh axis runs over, the one named last changes fastest.
Arguments:
- draft_features: bfloat16 [2048, 8192], P(('grp', 'seq'), 'head'), parts along dimension 0, may hold values from -6 to 6
- w_key: bfloat16 [8192, 1024], P(None, 'head'), may hold values from -0.0625 to 0.0625
- w_value: bfloat16 [8192, 1024], P(None, 'head'), may hold values from -0.0625 to 0.0625
- accepted: int32 [256], P(('grp', 'seq')), parts along dimension 0, may hold values from 1 to 8
- owner_group: int32 [256], P(('grp', 'seq')), parts along dimension 0, may hold values from 0 to 3, as said below
- page_slot: int32 [256], P(('grp', 'seq')), parts along dimension 0, may hold values from 0 to 63, as said below
Outputs:
- key_cache: bfloat16 [512, 8, 1024], P(('grp', 'seq'), None, 'head'), parts along dimension 0
- value_cache: bfloat16 [512, 8, 1024], P(('grp', 'seq'), None, 'head'), parts along dimension 0
There are 2 independent parts, one for each index of `grp`. A program takes and returns all parts, laid end to end along the dimension named above; an argument that names none is the same for every part. Nothing has to cross between parts.
Inputs may be any that keep to these rules, and one draw needn't show every extreme that they name: `owner_group`: the requests of one index of seq go to exactly 2 distinct owners, 16 to each; some owner receives 64 requests. `page_slot`: the requests of one owner have distinct slots.
All inputs are finite; a program needn't handle non-finite values.
Results may differ from a plain program's by a relative error of at most 0.001.
Values may be sent and summed in bfloat16 or wider, within the bound.
A program may use at most 64 MiB of HBM per device.

v0:
```python
import jax
import jax.numpy as jnp
from jax import lax
from jax.sharding import PartitionSpec as P


def pair_slots(owner_ids, slot_cap):
    row_count = owner_ids.shape[-1]
    same_owner = owner_ids[..., :, None] == owner_ids[..., None, :]
    before = lax.broadcasted_iota(jnp.int32, (row_count, row_count), 1) < lax.broadcasted_iota(
        jnp.int32, (row_count, row_count), 0
    )
    within = jnp.sum(jnp.where(same_owner & before, 1, 0), axis=-1).astype(jnp.int32)
    return owner_ids * slot_cap + within


def one_hot(labels, columns):
    return (
        labels[:, None] == lax.broadcasted_iota(jnp.int32, (labels.shape[0], columns), 1)
    ).astype(jnp.bfloat16)


def pack_rows(payload, slot_ids, slot_total):
    select = one_hot(slot_ids, slot_total)
    packed = lax.dot_general(
        select, payload, (((0,), (0,)), ((), ())), preferred_element_type=jnp.float32
    )
    return packed.astype(jnp.bfloat16)


def placement(all_owner, all_page, owner_self, req_dev, slot_cap, seq_count):
    slot_total = slot_cap * seq_count
    slot_ids = pair_slots(all_owner.reshape(seq_count, req_dev), slot_cap).reshape(-1)
    source = lax.broadcasted_iota(jnp.int32, (seq_count, req_dev), 0).reshape(-1)
    column = source * slot_cap + slot_ids - all_owner * slot_cap
    target = jnp.where(all_owner == owner_self, all_page, -1)
    to_page = one_hot(target, slot_total)
    from_column = one_hot(column, slot_total)
    placing = lax.dot_general(
        to_page, from_column, (((0,), (0,)), ((), ())), preferred_element_type=jnp.float32
    )
    return placing.astype(jnp.bfloat16)


def local(draft_features, w_key, w_value, accepted, owner_group, page_slot):
    req_dev = accepted.shape[0]
    draft_rows = draft_features.shape[0] // req_dev
    head_cols = w_key.shape[1]
    seq_count = lax.axis_size("seq")
    owner_self = lax.axis_index("seq")
    slot_cap = max(2, 2 * req_dev // seq_count)
    slot_total = slot_cap * seq_count
    send_slots = pair_slots(owner_group, slot_cap)
    live_rows = lax.broadcasted_iota(jnp.int32, (req_dev, draft_rows), 1) < accepted[:, None]
    all_owner, all_page = (
        lax.all_gather(owner_group, "seq", axis=0, tiled=True),
        lax.all_gather(page_slot, "seq", axis=0, tiled=True),
    )
    placing = placement(all_owner, all_page, owner_self, req_dev, slot_cap, seq_count)
    portion = lax.all_gather(draft_features, "head", axis=1, tiled=True)
    key_sum = jnp.dot(portion, w_key, preferred_element_type=jnp.float32)
    value_sum = jnp.dot(portion, w_value, preferred_element_type=jnp.float32)
    key_local = jnp.where(
        live_rows[:, :, None], key_sum.reshape(req_dev, draft_rows, head_cols), 0.0
    )
    value_local = jnp.where(
        live_rows[:, :, None], value_sum.reshape(req_dev, draft_rows, head_cols), 0.0
    )
    key_local = key_local.astype(jnp.bfloat16).reshape(req_dev, draft_rows * head_cols)
    value_local = value_local.astype(jnp.bfloat16).reshape(req_dev, draft_rows * head_cols)
    key_send = pack_rows(key_local, send_slots, slot_total)
    value_send = pack_rows(value_local, send_slots, slot_total)
    key_arrived, value_arrived = (
        lax.all_to_all(key_send, "seq", split_axis=0, concat_axis=0, tiled=True),
        lax.all_to_all(value_send, "seq", split_axis=0, concat_axis=0, tiled=True),
    )
    key_cache = jnp.dot(placing, key_arrived, preferred_element_type=jnp.float32).astype(
        jnp.bfloat16
    )
    value_cache = jnp.dot(placing, value_arrived, preferred_element_type=jnp.float32).astype(
        jnp.bfloat16
    )
    return (
        key_cache.reshape(slot_total, draft_rows, head_cols),
        value_cache.reshape(slot_total, draft_rows, head_cols),
    )


def solution(mesh):
    placed = (
        P(("grp", "seq"), "head"),
        P(None, "head"),
        P(None, "head"),
        P(("grp", "seq")),
        P(("grp", "seq")),
        P(("grp", "seq")),
    )
    return jax.shard_map(
        local,
        mesh=mesh,
        in_specs=placed,
        out_specs=(P(("grp", "seq"), None, "head"), P(("grp", "seq"), None, "head")),
        check_vma=False,
    )
```

profile of v0, /device:TPU:0, one launch (start us, length us, event | category | flops | bytes accessed | tf_op | source)
XLA Modules:
  0.0 84.7 jit_solution(431942104099704447)
XLA Ops:
  7.2 0.0 all-gather.2.cloned.1.call-start
  7.2 0.7 all-gather.2.cloned.1.call-update
  7.9 1.2 %dynamic-slice = u32[1]{0:T(128)} dynamic-slice(u32[32]{0:T(128)} %constant.19, u32[]{:T(128)S(6)} %add.13), dynamic_slice_sizes={1} | dynamic-slice | bytes 12
  9.8 0.9 %dynamic-update-slice = s32[128]{0:T(128)S(1)} dynamic-update-slice(s32[128]{0:T(128)S(1)} %broadcast.31.clone, s32[32]{0:T(128)} %param.10, u32[]{:T(128)} %bitcast) | dynamic-update-slice | bytes 260
  10.7 0.8 dynamic-update-slice.1
  11.5 9.9 %all-reduce.2 = (s32[128]{0:T(128)S(1)}, s32[128]{0:T(128)S(1)}) all-reduce(s32[128]{0:T(128)S(1)} %dynamic-update-slice, s32[128]{0:T(128)S(1)} %dynamic-update-slice.1), channel_id=1, replica_groups=mesh['grp'=2,'seq'=4,'head'=4] {'seq'}, use_global_device_ids=true, to_apply=%add | all-reduce | flops 256 | bytes 2048
  21.4 0.1 eq.66
  21.5 0.1 mul.19
  21.6 0.2 select_reduce_fusion
  21.8 0.1 reduce_sum.21
  21.9 0.7 iota_compare_fusion.4
  22.7 0.1 broadcast_in_dim.53
  22.8 0.9 %select_reduce_fusion.1 = s32[32]{0:T(128)S(1)} fusion(s32[32]{0:T(128)} %param.10), kind=kLoop, calls=%fused_computation.16 | loop fusion | flops 5088 | bytes 256 | tf_op jit(solution)/shard_map/reduce_sum | solution.py:13
  23.7 0.7 multiply_add_fusion
  24.4 22.4 %all-gather.2.cloned.1.call-done = bf16[256,8192]{1,0:T(8,128)(2,1)} async-done(((bf16[256,2048]{1,0:T(8,128)(2,1)}), bf16[256,8192]{1,0:T(8,128)(2,1)}) %all-gather.2.cloned.1.call-update) | async-done | bytes 4194320 | tf_op jit(solution)/shard_map/all_gather | solution.py:60
  46.7 4.7 %fusion.9 = bf16[256,256]{1,0:T(8,128)(2,1)S(1)} fusion(bf16[256,8192]{1,0:T(8,128)(2,1)} %all-gather.2.cloned.1.call-done, bf16[8192,256]{1,0:T(8,128)(2,1)} %param.8), kind=kOutput, calls=%fused_computation.27 | convolution fusion | flops 1073741824 | bytes 8519680 | tf_op jit(solution)/shard_map/dot_general | solution.py:62
  51.5 0.1 reshape.67
  51.5 1.1 %convolution_convert_fusion.1 = bf16[64,2048]{1,0:T(8,128)(2,1)} fusion(pred[32,2048]{1,0:T(8,128)(4,1)S(1)} %bitcast.23, bf16[32,2048]{1,0:T(8,128)(2,1)S(1)} %reshape.67, s32[32]{0:T(128)S(1)} %multiply_add_fusion), kind=kOutput, calls=%fused_computation.1 | convolution fusion | flops 8587264 | bytes 458880 | tf_op jit(solution)/shard_map/dot_general | solution.py:25
  52.6 4.7 %all-to-all-start.1 = ((bf16[4,16,2048]{2,1,0:T(8,128)(2,1)}), bf16[4,16,2048]{2,1,0:T(8,128)(2,1)S(1)}, u32[]{:S(2)}, u32[]{:S(2)}) async-start(bf16[4,16,2048]{2,1,0:T(8,128)(2,1)} %bitcast.3), calls=%async_computation.1 | async-start | bytes 524288 | tf_op jit(solution)/shard_map/all_to_all | solution.py:75
  57.2 4.7 %fusion.8 = bf16[256,256]{1,0:T(8,128)(2,1)S(1)} fusion(bf16[256,8192]{1,0:T(8,128)(2,1)} %all-gather.2.cloned.1.call-done, bf16[8192,256]{1,0:T(8,128)(2,1)} %param.7), kind=kOutput, calls=%fused_computation.26 | convolution fusion | flops 1073741824 | bytes 8519680 | tf_op jit(solution)/shard_map/dot_general | solution.py:61
  62.0 0.1 reshape.65
  62.0 1.1 %convolution_convert_fusion.3 = bf16[64,2048]{1,0:T(8,128)(2,1)} fusion(pred[32,2048]{1,0:T(8,128)(4,1)S(1)} %bitcast.24, bf16[32,2048]{1,0:T(8,128)(2,1)S(1)} %reshape.65, s32[32]{0:T(128)S(1)} %multiply_add_fusion), kind=kOutput, calls=%fused_computation.3 | convolution fusion | flops 8587264 | bytes 458880 | tf_op jit(solution)/shard_map/dot_general | solution.py:25
  63.1 3.5 %all-to-all-done.1 = bf16[4,16,2048]{2,1,0:T(8,128)(2,1)S(1)} async-done(((bf16[4,16,2048]{2,1,0:T(8,128)(2,1)}), bf16[4,16,2048]{2,1,0:T(8,128)(2,1)S(1)}, u32[]{:S(2)}, u32[]{:S(2)}) %all-to-all-start.1) | async-done | bytes 262176 | tf_op jit(solution)/shard_map/all_to_all | solution.py:75
  66.6 3.4 %all-to-all-start = ((bf16[4,16,2048]{2,1,0:T(8,128)(2,1)}), bf16[4,16,2048]{2,1,0:T(8,128)(2,1)S(1)}, u32[]{:S(2)}, u32[]{:S(2)}) async-start(bf16[4,16,2048]{2,1,0:T(8,128)(2,1)} %bitcast.1), calls=%async_computation | async-start | bytes 524288 | tf_op jit(solution)/shard_map/all_to_all | solution.py:74
  70.0 0.3 convolution_convert_fusion.4
  70.2 0.2 convolution_convert_fusion
  70.5 0.8 copy.10
  71.2 5.7 %all-to-all-done = bf16[4,16,2048]{2,1,0:T(8,128)(2,1)S(1)} async-done(((bf16[4,16,2048]{2,1,0:T(8,128)(2,1)}), bf16[4,16,2048]{2,1,0:T(8,128)(2,1)S(1)}, u32[]{:S(2)}, u32[]{:S(2)}) %all-to-all-start) | async-done | bytes 262176 | tf_op jit(solution)/shard_map/all_to_all | solution.py:74
  76.9 0.2 convolution_convert_fusion.2
  77.1 0.8 copy.9
  (6 shorter events, 0.1 us)
Async XLA Ops:
  7.2 39.6 %all-gather.2.cloned.1.call-start = ((), (), s32[]{:S(2)}) async-start(), calls=%async_computation.2 | async-start | bytes 5242880 | tf_op jit(solution)/shard_map/all_gather | solution.py:60
  52.6 14.0 %all-to-all-start.1 = ((bf16[4,16,2048]{2,1,0:T(8,128)(2,1)}), bf16[4,16,2048]{2,1,0:T(8,128)(2,1)S(1)}, u32[]{:S(2)}, u32[]{:S(2)}) async-start(bf16[4,16,2048]{2,1,0:T(8,128)(2,1)} %bitcast.3), calls=%async_computation.1 | async-start | bytes 524288 | tf_op jit(solution)/shard_map/all_to_all | solution.py:75
  66.6 10.3 %all-to-all-start = ((bf16[4,16,2048]{2,1,0:T(8,128)(2,1)}), bf16[4,16,2048]{2,1,0:T(8,128)(2,1)S(1)}, u32[]{:S(2)}, u32[]{:S(2)}) async-start(bf16[4,16,2048]{2,1,0:T(8,128)(2,1)} %bitcast.1), calls=%async_computation | async-start | bytes 524288 | tf_op jit(solution)/shard_map/all_to_all | solution.py:74
Sparse Core Ops, SparseCore 0:
  9.5 37.1 all-gather.1
where the time goes:
time: 85.1 us; the launch traced here: 84.7 us
  waiting for transfers between devices  32.2 us (38%)
  between operations  14.8 us (17%)
  matrix products  12.2 us (14%)
  blocking collectives  9.92 us (12%)
  starting transfers between devices  8.1 us (10%)
  local copies, waits for them, and re-layouts  4.98 us (6%)
  other arithmetic  2.55 us (3%)
    all_gather x1, waiting for transfers between devices, local(): portion = lax.all_gather(draft_features, 'head', axis=1, tiled=True)  22.4 us
    unnamed x1, blocking collectives  9.92 us
    all_to_all x1, waiting for transfers between devices, local(): lax.all_to_all(key_send, 'seq', split_axis=0, concat_axis=0, tiled=True)  5.69 us
    dot_general x1, matrix products, local(): value_sum = jnp.dot(portion, w_value, preferred_element_type=jnp.float32)  4.71 us
    dot_general x1, matrix products, local(): key_sum = jnp.dot(portion, w_key, preferred_element_type=jnp.float32)  4.71 us
    all_to_all x1, starting transfers between devices, local(): lax.all_to_all(value_send, 'seq', split_axis=0, concat_axis=0, tiled=True)  4.65 us
    unnamed x8, local copies, waits for them, and re-layouts  4.49 us
    all_to_all x1, waiting for transfers between devices, local(): lax.all_to_all(value_send, 'seq', split_axis=0, concat_axis=0, tiled=True)  3.47 us
  transfers between devices with their start and end apart: 3, of which 3 were waited for; matrix products, arithmetic and copies ran while one was open for 15% of the time, Pallas kernels for 0%

commit v1 on v0

--- a/solution.py
+++ b/solution.py
@@ -2,6 +2,7 @@
 import jax.numpy as jnp
 from jax import lax
 from jax.sharding import PartitionSpec as P
+from jax.lax import axis_index, axis_size, ppermute
 
 
 def pair_slots(owner_ids, slot_cap):
@@ -57,7 +58,20 @@
         lax.all_gather(page_slot, "seq", axis=0, tiled=True),
     )
     placing = placement(all_owner, all_page, owner_self, req_dev, slot_cap, seq_count)
-    portion = lax.all_gather(draft_features, "head", axis=1, tiled=True)
+
+    def _direct_views(local_values, comm_axis):
+        cores_n = axis_size(comm_axis)
+        later = sorted(((ix, (ix + 1) % cores_n) for ix in range(cores_n)))
+        field_out = local_values
+        all_rows = [field_out]
+        for rr in range(1, cores_n):
+            field_out = ppermute(field_out, comm_axis, later)
+            all_rows.insert(0, field_out)
+        value_now = jnp.concatenate(all_rows, axis=1)
+        part_next = axis_index(comm_axis) + 1
+        return jnp.roll(value_now, shift=part_next * local_values.shape[1], axis=1)
+
+    portion = _direct_views(draft_features, "head")
     key_sum = jnp.dot(portion, w_key, preferred_element_type=jnp.float32)
     value_sum = jnp.dot(portion, w_value, preferred_element_type=jnp.float32)
     key_local = jnp.where(

time: 85.1 us -> 80.7 us (0.948)
  between operations: 14.8 us -> 1.46 us
  local copies, waits for them, and re-layouts: 4.98 us -> 12.7 us
  waiting for transfers between devices: 32.2 us -> 37.6 us
  matrix products: 12.2 us -> 8.73 us
    ppermute x0 -> x3, waiting for transfers between devices: none -> 28.8 us  [_direct_views(): field_out = ppermute(field_out, comm_axis, later)]
    all_gather x1 -> x0, waiting for transfers between devices: 22.4 us -> none  [local(): portion = lax.all_gather(draft_features, 'head', axis=1, tiled=True)]
    unnamed x8 -> x21, local copies, waits for them, and re-layouts: 4.49 us -> 12.2 us
    dot_general x1, matrix products: 4.71 us -> 1.24 us  [local(): value_sum = jnp.dot(portion, w_value, preferred_element_type=jnp.float32)]
  transfers between devices with their start and end apart: 3 -> 5, of which waited for: 3 -> 4; matrix products, arithmetic and copies ran while one was open for 15% -> 16% of each run, Pallas kernels for 0% -> 0%
where the time goes in v1:
time: 80.7 us; the launch traced here: 80.3 us
  waiting for transfers between devices  37.6 us (47%)
  local copies, waits for them, and re-layouts  12.7 us (16%)
  blocking collectives  9.24 us (11%)
  matrix products  8.73 us (11%)
  starting transfers between devices  8 us (10%)
  other arithmetic  2.55 us (3%)
  between operations  1.46 us (2%)
    ppermute x3, waiting for transfers between devices, _direct_views(): field_out = ppermute(field_out, comm_axis, later)  28.8 us
    unnamed x21, local copies, waits for them, and re-layouts  12.2 us
    unnamed x1, blocking collectives  9.24 us
    all_to_all x1, waiting for transfers between devices, local(): lax.all_to_all(key_send, 'seq', split_axis=0, concat_axis=0, tiled=True)  5.76 us
    dot_general x1, matrix products, local(): key_sum = jnp.dot(portion, w_key, preferred_element_type=jnp.float32)  4.71 us
    all_to_all x1, starting transfers between devices, local(): lax.all_to_all(value_send, 'seq', split_axis=0, concat_axis=0, tiled=True)  4.02 us
    all_to_all x1, starting transfers between devices, local(): lax.all_to_all(key_send, 'seq', split_axis=0, concat_axis=0, tiled=True)  3.41 us
    all_to_all x1, waiting for transfers between devices, local(): lax.all_to_all(value_send, 'seq', split_axis=0, concat_axis=0, tiled=True)  3 us
  transfers between devices with their start and end apart: 5, of which 4 were waited for; matrix products, arithmetic and copies ran while one was open for 16% of the time, Pallas kernels for 0%

profile of v1, /device:TPU:0, one launch (start us, length us, event | category | flops | bytes accessed | tf_op | source)
XLA Modules:
  0.0 80.3 jit_solution(674749974030584863)
XLA Ops:
  0.6 0.5 collective-permute-start
  1.2 14.6 %collective-permute-done = bf16[256,2048]{1,0:T(8,128)(2,1)S(1)} collective-permute-done((bf16[256,2048]{1,0:T(8,128)(2,1)}, bf16[256,2048]{1,0:T(8,128)(2,1)S(1)}, u32[]{:S(2)}, u32[]{:S(2)}) %collective-permute-start) | collective-permute-done | bytes 1048608 | tf_op jit(solution)/shard_map/ppermute | solution.py:68
  15.8 14.2 %collective-permute-done.1 = bf16[256,2048]{1,0:T(8,128)(2,1)S(1)} collective-permute-done((bf16[256,2048]{1,0:T(8,128)(2,1)S(1)}, bf16[256,2048]{1,0:T(8,128)(2,1)S(1)}, u32[]{:S(2)}, u32[]{:S(2)}) %collective-permute-start.1) | collective-permute-done | bytes 1048608 | tf_op jit(solution)/shard_map/ppermute | solution.py:68
  30.0 0.7 iota_compare_fusion.4
  30.8 0.1 broadcast_in_dim.53
  30.9 1.2 %dynamic-slice = u32[1]{0:T(128)} dynamic-slice(u32[32]{0:T(128)} %constant.44, u32[]{:T(128)S(6)} %add.29), dynamic_slice_sizes={1} | dynamic-slice | bytes 12
  32.8 0.9 %dynamic-update-slice = s32[128]{0:T(128)S(1)} dynamic-update-slice(s32[128]{0:T(128)S(1)} %broadcast.32.clone, s32[32]{0:T(128)} %param.10, u32[]{:T(128)} %bitcast) | dynamic-update-slice | bytes 260
  33.7 0.8 %dynamic-update-slice.1 = s32[128]{0:T(128)S(1)} dynamic-update-slice(s32[128]{0:T(128)S(1)} %broadcast.32.clone.1, s32[32]{0:T(128)} %param.11, u32[]{:T(128)} %bitcast) | dynamic-update-slice | bytes 260
  34.5 9.2 %all-reduce.2 = (s32[128]{0:T(128)S(1)}, s32[128]{0:T(128)S(1)}) all-reduce(s32[128]{0:T(128)S(1)} %dynamic-update-slice, s32[128]{0:T(128)S(1)} %dynamic-update-slice.1), channel_id=1, replica_groups=mesh['grp'=2,'seq'=4,'head'=4] {'seq'}, use_global_device_ids=true, to_apply=%add | all-reduce | flops 256 | bytes 2048
  43.9 0.2 select_reduce_fusion
  44.3 0.9 %select_reduce_fusion.1 = s32[32]{0:T(128)S(1)} fusion(s32[32]{0:T(128)} %param.10), kind=kLoop, calls=%fused_computation.28 | loop fusion | flops 5088 | bytes 256 | tf_op jit(solution)/shard_map/reduce_sum | solution.py:14
  45.2 0.7 multiply_add_fusion
  45.9 1.4 %constant_dynamic-update-slice_fusion.7 = bf16[256,16384]{1,0:T(8,128)(2,1)S(1)} fusion(bf16[256,2048]{1,0:T(8,128)(2,1)} %collective-permute-done.2), kind=kLoop, calls=%fused_computation.25 | loop fusion | bytes 2097152
  47.4 0.1 constant_dynamic-update-slice_fusion.5
  47.5 1.3 %constant_dynamic-update-slice_fusion.4 = bf16[256,16384]{1,0:T(8,128)(2,1)S(1)} fusion(bf16[256,16384]{1,0:T(8,128)(2,1)S(1)} %constant_dynamic-update-slice_fusion.5, bf16[256,2048]{1,0:T(8,128)(2,1)} %param.6), kind=kLoop, calls=%fused_computation.22 | loop fusion | bytes 2097152
  48.8 1.3 %constant_dynamic-update-slice_fusion.3 = bf16[256,16384]{1,0:T(8,128)(2,1)S(1)} fusion(bf16[256,16384]{1,0:T(8,128)(2,1)S(1)} %constant_dynamic-update-slice_fusion.4, bf16[256,2048]{1,0:T(8,128)(2,1)} %collective-permute-done.2), kind=kLoop, calls=%fused_computation.21 | loop fusion | bytes 2097152
  50.1 0.1 constant_dynamic-update-slice_fusion.2
  50.2 0.1 constant_dynamic-update-slice_fusion.1
  50.5 3.2 %copy-done.1 = bf16[256,16384]{1,0:T(8,128)(2,1)} copy-done((bf16[256,16384]{1,0:T(8,128)(2,1)}, bf16[256,16384]{1,0:T(8,128)(2,1)S(1)}, u32[]{:S(2)}) %copy-start.1) | copy-done | bytes 8388632
  53.7 1.2 %fusion = bf16[256,256]{1,0:T(8,128)(2,1)S(1)} fusion(bf16[8192,256]{1,0:T(8,128)(2,1)S(1)} %copy-done.2, bf16[256,16384]{1,0:T(8,128)(2,1)S(1)} %constant_dynamic-update-slice_fusion, s32[]{:T(128)S(6)} %select_n.38), kind=kOutput, calls=%fused_computation | convolution fusion | flops 1073741824 | bytes 8519684 | tf_op jit(solution)/shard_map/dot_general | solution.py:76
  55.0 1.0 %convolution_convert_fusion.1 = bf16[64,2048]{1,0:T(8,128)(2,1)} fusion(pred[32,2048]{1,0:T(8,128)(4,1)S(1)} %bitcast.21, bf16[32,2048]{1,0:T(8,128)(2,1)S(1)} %reshape.67, s32[32]{0:T(128)S(1)} %multiply_add_fusion), kind=kOutput, calls=%fused_computation.5 | convolution fusion | flops 8587264 | bytes 458880 | tf_op jit(solution)/shard_map/dot_general | solution.py:26
  56.1 4.0 %all-to-all-start.1 = ((bf16[4,16,2048]{2,1,0:T(8,128)(2,1)}), bf16[4,16,2048]{2,1,0:T(8,128)(2,1)S(1)}, u32[]{:S(2)}, u32[]{:S(2)}) async-start(bf16[4,16,2048]{2,1,0:T(8,128)(2,1)} %bitcast.3), calls=%async_computation.1 | async-start | bytes 524288 | tf_op jit(solution)/shard_map/all_to_all | solution.py:89
  60.1 4.7 %fusion.2 = bf16[256,256]{1,0:T(8,128)(2,1)S(1)} fusion(bf16[8192,256]{1,0:T(8,128)(2,1)} %param.7, bf16[256,16384]{1,0:T(8,128)(2,1)} %copy-done.1, s32[]{:T(128)S(6)} %select_n.38), kind=kOutput, calls=%fused_computation.2 | convolution fusion | flops 1073741824 | bytes 8519684 | tf_op jit(solution)/shard_map/dot_general | solution.py:75
  64.9 1.0 %convolution_convert_fusion.3 = bf16[64,2048]{1,0:T(8,128)(2,1)} fusion(pred[32,2048]{1,0:T(8,128)(4,1)S(1)} %bitcast.22, bf16[32,2048]{1,0:T(8,128)(2,1)S(1)} %reshape.65, s32[32]{0:T(128)S(1)} %multiply_add_fusion), kind=kOutput, calls=%fused_computation.7 | convolution fusion | flops 8587264 | bytes 458880 | tf_op jit(solution)/shard_map/dot_general | solution.py:26
  65.9 3.0 %all-to-all-done.1 = bf16[4,16,2048]{2,1,0:T(8,128)(2,1)S(1)} async-done(((bf16[4,16,2048]{2,1,0:T(8,128)(2,1)}), bf16[4,16,2048]{2,1,0:T(8,128)(2,1)S(1)}, u32[]{:S(2)}, u32[]{:S(2)}) %all-to-all-start.1) | async-done | bytes 262176 | tf_op jit(solution)/shard_map/all_to_all | solution.py:89
  68.9 3.4 %all-to-all-start = ((bf16[4,16,2048]{2,1,0:T(8,128)(2,1)}), bf16[4,16,2048]{2,1,0:T(8,128)(2,1)S(1)}, u32[]{:S(2)}, u32[]{:S(2)}) async-start(bf16[4,16,2048]{2,1,0:T(8,128)(2,1)} %bitcast.1), calls=%async_computation | async-start | bytes 524288 | tf_op jit(solution)/shard_map/all_to_all | solution.py:88
  72.3 0.3 convolution_convert_fusion.4
  72.6 0.2 convolution_convert_fusion
  72.8 0.8 copy.10
  73.6 5.8 %all-to-all-done = bf16[4,16,2048]{2,1,0:T(8,128)(2,1)S(1)} async-done(((bf16[4,16,2048]{2,1,0:T(8,128)(2,1)}), bf16[4,16,2048]{2,1,0:T(8,128)(2,1)S(1)}, u32[]{:S(2)}, u32[]{:S(2)}) %all-to-all-start) | async-done | bytes 262176 | tf_op jit(solution)/shard_map/all_to_all | solution.py:88
  79.3 0.2 convolution_convert_fusion.2
  79.6 0.8 copy.9
  (21 shorter events, 0.7 us)
Async XLA Ops:
  0.6 49.7 %copy-start = (bf16[256,2048]{1,0:T(8,128)(2,1)S(1)}, bf16[256,2048]{1,0:T(8,128)(2,1)}, u32[]{:S(2)}) copy-start(bf16[256,2048]{1,0:T(8,128)(2,1)} %param.6) | copy-start | bytes 3145732
  0.6 15.2 %collective-permute-start = (bf16[256,2048]{1,0:T(8,128)(2,1)}, bf16[256,2048]{1,0:T(8,128)(2,1)S(1)}, u32[]{:S(2)}, u32[]{:S(2)}) collective-permute-start(bf16[256,2048]{1,0:T(8,128)(2,1)} %param.6), channel_id=1, source_target_pairs={{0,1},{1,2},{2,3},{3,0},{4,5},{5,6},{6,7},{7,4},{8,9},{9,10},{10,1... | collective-permute-start | bytes 3145736 | tf_op jit(solution)/shard_map/ppermute | solution.py:68
  15.8 14.2 %collective-permute-start.1 = (bf16[256,2048]{1,0:T(8,128)(2,1)S(1)}, bf16[256,2048]{1,0:T(8,128)(2,1)S(1)}, u32[]{:S(2)}, u32[]{:S(2)}) collective-permute-start(bf16[256,2048]{1,0:T(8,128)(2,1)S(1)} %collective-permute-done), channel_id=1, source_target_pairs={{0,1},{1,2},{2,3},{3,0},{4,5},{5,6},{6,7},{7,4},{8,9},{9,10},{10,1... | collective-permute-start | bytes 3145736 | tf_op jit(solution)/shard_map/ppermute | solution.py:68
  30.0 15.8 %collective-permute-start.2 = (bf16[256,2048]{1,0:T(8,128)(2,1)S(1)}, bf16[256,2048]{1,0:T(8,128)(2,1)}, u32[]{:S(2)}, u32[]{:S(2)}) collective-permute-start(bf16[256,2048]{1,0:T(8,128)(2,1)S(1)} %collective-permute-done.1), channel_id=1, source_target_pairs={{0,1},{1,2},{2,3},{3,0},{4,5},{5,6},{6,7},{7,4},{8,9},{9,10},{10,1... | collective-permute-start | bytes 3145736 | tf_op jit(solution)/shard_map/ppermute | solution.py:68
  45.9 7.8 %copy-start.2 = (bf16[8192,256]{1,0:T(8,128)(2,1)S(1)}, bf16[8192,256]{1,0:T(8,128)(2,1)}, u32[]{:S(2)}) copy-start(bf16[8192,256]{1,0:T(8,128)(2,1)} %param.8) | copy-start | bytes 12582916
  50.5 3.2 %copy-start.1 = (bf16[256,16384]{1,0:T(8,128)(2,1)}, bf16[256,16384]{1,0:T(8,128)(2,1)S(1)}, u32[]{:S(2)}) copy-start(bf16[256,16384]{1,0:T(8,128)(2,1)S(1)} %constant_dynamic-update-slice_fusion) | copy-start | bytes 25165828
  56.1 12.8 %all-to-all-start.1 = ((bf16[4,16,2048]{2,1,0:T(8,128)(2,1)}), bf16[4,16,2048]{2,1,0:T(8,128)(2,1)S(1)}, u32[]{:S(2)}, u32[]{:S(2)}) async-start(bf16[4,16,2048]{2,1,0:T(8,128)(2,1)} %bitcast.3), calls=%async_computation.1 | async-start | bytes 524288 | tf_op jit(solution)/shard_map/all_to_all | solution.py:89
  68.9 10.4 %all-to-all-start = ((bf16[4,16,2048]{2,1,0:T(8,128)(2,1)}), bf16[4,16,2048]{2,1,0:T(8,128)(2,1)S(1)}, u32[]{:S(2)}, u32[]{:S(2)}) async-start(bf16[4,16,2048]{2,1,0:T(8,128)(2,1)} %bitcast.1), calls=%async_computation | async-start | bytes 524288 | tf_op jit(solution)/shard_map/all_to_all | solution.py:88
